TPU v7x, 32 devices: a whole 2x2x4 slice. The times are simulated.
32 devices in a mesh: group: 4 (over y, core), dev: 8 (over z, x).
Axes of the slice: x: 2, y: 2, z: 4, core: 2. Of those that a mesh axis runs over, the one named last changes fastest.
Arguments:
- solution: float32 [4, 16, 16, 512], P('group', 'dev'), may hold values from -6 to 6
- residual: float32 [4, 16, 16, 512], P('group', 'dev'), may hold values from -6 to 6
- direction: float32 [4, 16, 16, 512], P('group', 'dev'), may hold values from -0.03 to 0.03
- geometry: bfloat16 [3, 4, 16, 16, 512], P(None, 'group', 'dev'), may hold values from 0.5 to 2
- mass: bfloat16 [4, 16, 16, 512], P('group', 'dev'), may hold values from 50 to 500
Outputs:
- solution_out: float32 [4, 16, 16, 512], P('group', 'dev')
- residual_out: float32 [4, 16, 16, 512], P('group', 'dev')
- direction_out: float32 [4, 16, 16, 512], P('group', 'dev')
All inputs are finite; a program needn't handle non-finite values.
Results may differ from a plain program's by a relative error of at most 0.0003.
Values sent between devices are 32-bit elements; how exact they have to be, the bound alone decides.
A program may use at most 64 MiB of HBM per device.

v0:
```python
import jax
import jax.numpy as jnp
import numpy as np
from jax import lax
from jax.sharding import PartitionSpec as P

NP = 8


lobatto_nodes = [
    -1.0,
    -0.8717401485096066,
    -0.5917001814331423,
    -0.2092992179024789,
    0.2092992179024789,
    0.5917001814331423,
    0.8717401485096066,
    1.0,
]


def extended(value, sides, width):
    for axis, dim in sides:
        peers, length = (lax.axis_size(axis), value.shape[dim])
        up = [(i, (i + 1) % peers) for i in range(peers)]
        down = [(j, i) for i, j in up]
        last = lax.slice_in_dim(value, length - width, length, axis=dim)
        initial = lax.slice_in_dim(value, 0, width, axis=dim)
        before = lax.ppermute(last, axis, up)
        after = lax.ppermute(initial, axis, down)
        value = jnp.concatenate([before, value, after], axis=dim)
    return value


def derivative_table():
    nodes = np.array(lobatto_nodes)
    identity = np.eye(NP)
    offset = nodes[:, None] - nodes[None, :] + identity
    barycentric = 1.0 / np.prod(offset, axis=1)
    derivative = barycentric[None, :] / barycentric[:, None] / offset * (1.0 - identity)
    return derivative - identity * np.sum(derivative, axis=1)[:, None]


def operator_tables():
    derivative = derivative_table()
    identity = np.eye(NP)
    kron_list = [
        np.kron(np.kron(derivative, identity), identity),
        np.kron(np.kron(identity, derivative), identity),
        np.kron(np.kron(identity, identity), derivative),
    ]
    forward = np.concatenate([matrix.T for matrix in kron_list], axis=1)
    backward = np.concatenate(kron_list, axis=0)
    squares = np.concatenate([matrix * matrix for matrix in kron_list], axis=0)
    return (
        jnp.asarray(forward, dtype=jnp.float32),
        jnp.asarray(backward, dtype=jnp.float32),
        jnp.asarray(squares, dtype=jnp.float32),
    )


def point_weights():
    edge = np.where(np.arange(NP) % (NP - 1) == 0, 0.5, 1.0)
    return jnp.asarray(np.kron(np.kron(edge, edge), edge), dtype=jnp.float32)


def highest(left, right):
    return jnp.dot(left, right, precision=lax.Precision.HIGHEST, preferred_element_type=jnp.float32)


def combine_faces(field, lower, upper, prev_upper, next_lower, elem_dim, node_dim):
    extent = field.shape[elem_dim]
    lower_next = jnp.concatenate(
        [lax.slice_in_dim(lower, 1, extent, axis=elem_dim), next_lower], axis=elem_dim
    )
    summed = upper + lower_next
    leading = prev_upper + lax.slice_in_dim(lower, 0, 1, axis=elem_dim)
    new_lower = jnp.concatenate(
        [leading, lax.slice_in_dim(summed, 0, extent - 1, axis=elem_dim)], axis=elem_dim
    )
    middle = lax.slice_in_dim(field, 1, NP - 1, axis=node_dim)
    return jnp.concatenate([new_lower, middle, summed], axis=node_dim)


def local_pass(field, elem_dim, node_dim, prev_upper, next_lower):
    lower = lax.index_in_dim(field, 0, node_dim, keepdims=True)
    upper = lax.index_in_dim(field, NP - 1, node_dim, keepdims=True)
    return combine_faces(field, lower, upper, prev_upper, next_lower, elem_dim, node_dim)


def group_pass(field):
    lower = lax.index_in_dim(field, 0, 4, keepdims=True)
    upper = lax.index_in_dim(field, NP - 1, 4, keepdims=True)
    extent = field.shape[1]
    end_faces = jnp.concatenate(
        [
            lax.slice_in_dim(lower, 0, 1, axis=1),
            lax.slice_in_dim(upper, extent - 1, extent, axis=1),
        ],
        axis=1,
    )
    padded = extended(end_faces, (("group", 1),), 1)
    return combine_faces(field, lower, upper, padded[:, 0:1], padded[:, 3:4], 1, 4)


def dev_neighbours(field):
    lower = lax.index_in_dim(field, 0, 5, keepdims=True)
    upper = lax.index_in_dim(field, NP - 1, 5, keepdims=True)
    extent = field.shape[2]
    end_faces = jnp.concatenate(
        [
            lax.slice_in_dim(lower, 0, 1, axis=2),
            lax.slice_in_dim(upper, extent - 1, extent, axis=2),
        ],
        axis=2,
    )
    padded = extended(end_faces, (("dev", 2),), 1)
    return (padded[:, :, 0:1], padded[:, :, 3:4])


def dev_pass(field):
    before, after = dev_neighbours(field)
    return local_pass(field, 2, 5, before, after)


def assemble(stacked):
    shaped = stacked.reshape(stacked.shape[:4] + (NP, NP, NP))
    shaped = dev_pass(group_pass(shaped))
    extent = shaped.shape[3]
    lower = lax.index_in_dim(shaped, 0, 6, keepdims=True)
    upper = lax.index_in_dim(shaped, NP - 1, 6, keepdims=True)
    shaped = combine_faces(
        shaped,
        lower,
        upper,
        lax.slice_in_dim(upper, extent - 1, extent, axis=3),
        lax.slice_in_dim(lower, 0, 1, axis=3),
        3,
        6,
    )
    return shaped.reshape(stacked.shape)


def on_device(solution, residual, direction, geometry, mass):
    forward, backward, squares = operator_tables()
    weights = point_weights()
    points = NP**3
    dims_full = solution.shape
    elements = dims_full[0] * dims_full[1] * dims_full[2]
    geometry_rows = jnp.moveaxis(geometry.astype(jnp.float32), 0, -2).reshape(elements, 3 * points)
    mass_coef = mass.astype(jnp.float32).reshape(elements, points)
    diag_local = (highest(geometry_rows, squares) + mass_coef).reshape(dims_full)
    both = assemble(jnp.stack([diag_local, weights * direction]))
    diagonal = both[0]
    smooth = both[1]
    flat = smooth.reshape(elements, points)
    fluxes = geometry_rows * highest(flat, forward)
    applied_local = highest(fluxes, backward) + mass_coef * flat
    applied = assemble(applied_local.reshape((1,) + dims_full))[0]
    scaled = residual / diagonal
    norm_now, curvature, cross_term, quad_term = lax.psum(
        (
            jnp.sum(weights * residual * scaled),
            jnp.sum(weights * smooth * applied),
            jnp.sum(weights * scaled * applied),
            jnp.sum(weights * applied * applied / diagonal),
        ),
        ("group", "dev"),
    )
    step_size = norm_now / curvature
    residual_out = residual - step_size * applied
    norm_next = norm_now - 2.0 * step_size * cross_term + step_size * step_size * quad_term
    solution_out = solution + step_size * smooth
    direction_out = residual_out / diagonal + norm_next / norm_now * smooth
    return (solution_out, residual_out, direction_out)


def solution(mesh):
    return jax.shard_map(
        on_device,
        mesh=mesh,
        in_specs=(
            P("group", "dev", None, None),
            P("group", "dev", None, None),
            P("group", "dev", None, None),
            P(None, "group", "dev", None, None),
            P("group", "dev", None, None),
        ),
        out_specs=(
            P("group", "dev", None, None),
            P("group", "dev", None, None),
            P("group", "dev", None, None),
        ),
        check_vma=False,
    )
```

profile of v0, /device:TPU:0, one launch (start us, length us, event | category | flops | bytes accessed | tf_op | source)
XLA Modules:
  0.0 103.6 jit_solution(4814848482912442824)
XLA Ops:
  0.6 1.0 copy.31
  1.7 3.1 %fusion = f32[32,512]{1,0:T(8,128)S(1)} fusion(f32[1536,512]{1,0:T(8,128)} %constant.14.clone, bf16[32,1536]{1,0:T(8,128)(2,1)S(1)} %bitcast.39, bf16[32,512]{1,0:T(8,128)(2,1)} %bitcast.43), kind=kOutput, calls=%fused_computation.7 | convolution fusion | flops 302022656 | bytes 3342336 | tf_op jit(solution)/shard_map/dot_general | solution.py:68
  4.9 0.3 stack.8
  5.7 0.5 collective-permute-start
  6.2 4.6 %collective-permute-done = f32[2,1,2,16,1,8,8]{3,6,5,4,2,1,0:T(8,128)S(1)} collective-permute-done((f32[2,1,2,16,1,8,8]{3,6,5,4,2,1,0:T(8,128)S(1)}, f32[2,1,2,16,1,8,8]{3,6,5,4,2,1,0:T(8,128)S(1)}, u32[]{:S(2)}, u32[]{:S(2)}) %collective-permute-start) | collective-permute-done | bytes 16416 | tf_op jit(solution)/shard_map/ppermute | solution.py:29
  10.9 2.5 %collective-permute-done.1 = f32[2,1,2,16,1,8,8]{3,6,5,4,2,1,0:T(8,128)S(1)} collective-permute-done((f32[2,1,2,16,1,8,8]{3,6,5,4,2,1,0:T(8,128)S(1)}, f32[2,1,2,16,1,8,8]{3,6,5,4,2,1,0:T(8,128)S(1)}, u32[]{:S(2)}, u32[]{:S(2)}) %collective-permute-start.1) | collective-permute-done | bytes 16416 | tf_op jit(solution)/shard_map/ppermute | solution.py:30
  13.6 2.3 %collective-permute-start.2 = (f32[2,1,1,16,8,1,8]{3,6,5,4,2,1,0:T(8,128)S(1)}, f32[2,1,1,16,8,1,8]{3,6,5,4,2,1,0:T(8,128)S(1)}, u32[]{:S(2)}, u32[]{:S(2)}) collective-permute-start(f32[2,1,1,16,8,1,8]{3,6,5,4,2,1,0:T(8,128)S(1)} %slice.154), channel_id=1, source_target_pairs={{0,1},{1,2},{2,3},{3,4},{4,5},{5,6},{6,7},{7,0},{8,9},{9,10},{10,1... | collective-permute-start | bytes 24584 | tf_op jit(solution)/shard_map/ppermute | solution.py:29
  15.9 5.3 %collective-permute-done.2 = f32[2,1,1,16,8,1,8]{3,6,5,4,2,1,0:T(8,128)S(1)} collective-permute-done((f32[2,1,1,16,8,1,8]{3,6,5,4,2,1,0:T(8,128)S(1)}, f32[2,1,1,16,8,1,8]{3,6,5,4,2,1,0:T(8,128)S(1)}, u32[]{:S(2)}, u32[]{:S(2)}) %collective-permute-start.2) | collective-permute-done | bytes 8224 | tf_op jit(solution)/shard_map/ppermute | solution.py:29
  21.2 2.1 %collective-permute-start.3 = (f32[2,1,1,16,8,1,8]{3,6,5,4,2,1,0:T(8,128)S(1)}, f32[2,1,1,16,8,1,8]{3,6,5,4,2,1,0:T(8,128)S(1)}, u32[]{:S(2)}, u32[]{:S(2)}) collective-permute-start(f32[2,1,1,16,8,1,8]{3,6,5,4,2,1,0:T(8,128)S(1)} %get-tuple-element.31), channel_id=1, source_target_pairs={{1,0},{2,1},{3,2},{4,3},{5,4},{6,5},{7,6},{0,7},{9,8},{10,9},{11,1... | collective-permute-start | bytes 24584 | tf_op jit(solution)/shard_map/ppermute | solution.py:30
  23.4 2.8 %collective-permute-done.3 = f32[2,1,1,16,8,1,8]{3,6,5,4,2,1,0:T(8,128)S(1)} collective-permute-done((f32[2,1,1,16,8,1,8]{3,6,5,4,2,1,0:T(8,128)S(1)}, f32[2,1,1,16,8,1,8]{3,6,5,4,2,1,0:T(8,128)S(1)}, u32[]{:S(2)}, u32[]{:S(2)}) %collective-permute-start.3) | collective-permute-done | bytes 8224 | tf_op jit(solution)/shard_map/ppermute | solution.py:30
  26.2 0.4 maximum_add_fusion
  26.6 0.6 fusion.13
  27.2 0.5 fusion.2
  27.8 0.4 copy.37
  28.2 0.3 reshape_squeeze.3
  28.6 4.0 %convolution_multiply_fusion = f32[32,1536]{1,0:T(8,128)S(1)} fusion(f32[32,512]{0,1:T(8,128)S(1)} %reshape_squeeze.3, f32[512,1536]{1,0:T(8,128)} %constant.12.clone, bf16[32,1536]{1,0:T(8,128)(2,1)S(1)} %bitcast.40), kind=kOutput, calls=%fused_computation | convolution fusion | flops 302088192 | bytes 3506176 | tf_op jit(solution)/shard_map/dot_general | solution.py:68
  32.6 1.9 %convolution_add_fusion = f32[32,512]{1,0:T(8,128)S(1)} fusion(f32[32,1536]{1,0:T(8,128)S(1)} %convolution_multiply_fusion, f32[1536,512]{1,0:T(8,128)S(1)} %copy-done, f32[32,512]{1,0:T(8,128)S(1)} %copy.38, bf16[32,512]{1,0:T(8,128)(2,1)S(1)} %bitcast.44), kind=kOutput, calls=%fused_computation.5 | convolution fusion | flops 302039040 | bytes 3506176 | tf_op jit(solution)/shard_map/dot_general | solution.py:68
  34.6 0.3 reshape_reshape.3
  35.1 3.7 %collective-permute-done.4 = f32[1,1,2,16,1,8,8]{3,6,5,4,2,1,0:T(8,128)S(1)} collective-permute-done((f32[1,1,2,16,1,8,8]{3,6,5,4,2,1,0:T(8,128)S(1)}, f32[1,1,2,16,1,8,8]{3,6,5,4,2,1,0:T(8,128)S(1)}, u32[]{:S(2)}, u32[]{:S(2)}) %collective-permute-start.4) | collective-permute-done | bytes 8224 | tf_op jit(solution)/shard_map/ppermute | solution.py:29
  38.9 1.8 %collective-permute-done.5 = f32[1,1,2,16,1,8,8]{3,6,5,4,2,1,0:T(8,128)S(1)} collective-permute-done((f32[1,1,2,16,1,8,8]{3,6,5,4,2,1,0:T(8,128)S(1)}, f32[1,1,2,16,1,8,8]{3,6,5,4,2,1,0:T(8,128)S(1)}, u32[]{:S(2)}, u32[]{:S(2)}) %collective-permute-start.5) | collective-permute-done | bytes 8224 | tf_op jit(solution)/shard_map/ppermute | solution.py:30
  40.8 6.6 %collective-permute-done.6 = f32[1,1,1,16,8,1,8]{3,6,5,4,2,1,0:T(8,128)S(1)} collective-permute-done((f32[1,1,1,16,8,1,8]{3,6,5,4,2,1,0:T(8,128)S(1)}, f32[1,1,1,16,8,1,8]{3,6,5,4,2,1,0:T(8,128)S(1)}, u32[]{:S(2)}, u32[]{:S(2)}) %collective-permute-start.6) | collective-permute-done | bytes 4128 | tf_op jit(solution)/shard_map/ppermute | solution.py:29
  47.4 1.8 %collective-permute-start.7 = (f32[1,1,1,16,8,1,8]{3,6,5,4,2,1,0:T(8,128)S(1)}, f32[1,1,1,16,8,1,8]{3,6,5,4,2,1,0:T(8,128)S(1)}, u32[]{:S(2)}, u32[]{:S(2)}) collective-permute-start(f32[1,1,1,16,8,1,8]{3,6,5,4,2,1,0:T(8,128)S(1)} %get-tuple-element.21), channel_id=1, source_target_pairs={{1,0},{2,1},{3,2},{4,3},{5,4},{6,5},{7,6},{0,7},{9,8},{10,9},{11,1... | collective-permute-start | bytes 12296 | tf_op jit(solution)/shard_map/ppermute | solution.py:30
  49.5 1.0 copy.36
  50.7 0.8 collective-permute-done.7
  52.2 1.1 %fusion.10 = (f32[]{:T(128)}, f32[]{:T(128)}, f32[1,1,2,16,8,8,8]{3,6,5,4,2,1,0:T(8,128)S(1)}, f32[1,1,2,16,8,8,8]{3,6,5,4,2,1,0:T(8,128)S(1)}) fusion(f32[8,8,8]{2,1,0:T(8,128)S(1)} %copy-done.7, f32[2,1,2,16,8,8,8]{3,6,5,4,2,1,0:T(8,128)S(1)} %fusion.2, f32[1,1,2,16,8,8,1]{3,6,5,4,2,1,0:T(1,128)S(1)} %slice_add_fusion.1, ...), kind=kLoop, calls=%fused_computation.32 | loop fusion | flops 163838 | bytes 329736 | tf_op jit(solution)/shard_map/reduce_sum | solution.py:166
  53.3 0.8 multiply_reduce_fusion
  54.2 40.2 %all-reduce = (f32[]{:T(128)}, f32[]{:T(128)}, f32[]{:T(128)}, f32[]{:T(128)}) all-reduce(f32[]{:T(128)} %get-tuple-element.12, f32[]{:T(128)} %get-tuple-element.10, f32[]{:T(128)} %get-tuple-element.11, f32[]{:T(128)} %get-tuple-element.9), channel_id=1, replica_groups=mesh['group'=4,'dev'=8] {'group','dev'}, use_global_device_ids=true, to_apply=%region_1.0 | all-reduce | flops 4 | bytes 32 | tf_op jit(solution)/shard_map/psum | solution.py:161
  98.3 0.9 broadcast_multiply_fusion
  99.2 0.9 divide_add_fusion
  100.1 1.8 %copy.46 = f32[1,2,16,512]{3,2,1,0:T(8,128)} copy(f32[1,2,16,512]{2,3,1,0:T(8,128)} %get-tuple-element.18) | data formatting | bytes 131072
  101.9 0.8 copy.47
  102.8 0.8 copy.45
  (58 shorter events, 2.6 us)
Async XLA Ops:
  0.6 4.7 %copy-start.5 = (f32[1,2,16,512]{3,2,1,0:T(8,128)S(1)}, f32[1,2,16,512]{3,2,1,0:T(8,128)}, u32[]{:S(2)}) copy-start(f32[1,2,16,512]{3,2,1,0:T(8,128)} %param.11) | copy-start | bytes 196612
  1.7 3.9 %copy-start.8 = (f32[512]{0:T(512)S(1)}, f32[512]{0:T(512)}, u32[]{:S(2)}) copy-start(f32[512]{0:T(512)} %constant.15.clone) | copy-start | bytes 6148
  5.7 5.1 %collective-permute-start = (f32[2,1,2,16,1,8,8]{3,6,5,4,2,1,0:T(8,128)S(1)}, f32[2,1,2,16,1,8,8]{3,6,5,4,2,1,0:T(8,128)S(1)}, u32[]{:S(2)}, u32[]{:S(2)}) collective-permute-start(f32[2,1,2,16,1,8,8]{3,6,5,4,2,1,0:T(8,128)S(1)} %pad_maximum_fusion.6), channel_id=1, source_target_pairs={{0,8},{8,16},{16,24},{24,0},{1,9},{9,17},{17,25},{25,1},{2,10},{10... | collective-permute-start | bytes 49160 | tf_op jit(solution)/shard_map/ppermute | solution.py:29
  10.9 2.6 %collective-permute-start.1 = (f32[2,1,2,16,1,8,8]{3,6,5,4,2,1,0:T(8,128)S(1)}, f32[2,1,2,16,1,8,8]{3,6,5,4,2,1,0:T(8,128)S(1)}, u32[]{:S(2)}, u32[]{:S(2)}) collective-permute-start(f32[2,1,2,16,1,8,8]{3,6,5,4,2,1,0:T(8,128)S(1)} %get-tuple-element.23), channel_id=1, source_target_pairs={{8,0},{16,8},{24,16},{0,24},{9,1},{17,9},{25,17},{1,25},{10,2},{18... | collective-permute-start | bytes 49160 | tf_op jit(solution)/shard_map/ppermute | solution.py:30
  13.6 7.6 %collective-permute-start.2 = (f32[2,1,1,16,8,1,8]{3,6,5,4,2,1,0:T(8,128)S(1)}, f32[2,1,1,16,8,1,8]{3,6,5,4,2,1,0:T(8,128)S(1)}, u32[]{:S(2)}, u32[]{:S(2)}) collective-permute-start(f32[2,1,1,16,8,1,8]{3,6,5,4,2,1,0:T(8,128)S(1)} %slice.154), channel_id=1, source_target_pairs={{0,1},{1,2},{2,3},{3,4},{4,5},{5,6},{6,7},{7,0},{8,9},{9,10},{10,1... | collective-permute-start | bytes 24584 | tf_op jit(solution)/shard_map/ppermute | solution.py:29
  21.2 4.9 %collective-permute-start.3 = (f32[2,1,1,16,8,1,8]{3,6,5,4,2,1,0:T(8,128)S(1)}, f32[2,1,1,16,8,1,8]{3,6,5,4,2,1,0:T(8,128)S(1)}, u32[]{:S(2)}, u32[]{:S(2)}) collective-permute-start(f32[2,1,1,16,8,1,8]{3,6,5,4,2,1,0:T(8,128)S(1)} %get-tuple-element.31), channel_id=1, source_target_pairs={{1,0},{2,1},{3,2},{4,3},{5,4},{6,5},{7,6},{0,7},{9,8},{10,9},{11,1... | collective-permute-start | bytes 24584 | tf_op jit(solution)/shard_map/ppermute | solution.py:30
  27.8 4.8 %copy-start.4 = (bf16[1,2,16,512]{3,2,1,0:T(8,128)(2,1)S(1)}, bf16[1,2,16,512]{3,2,1,0:T(8,128)(2,1)}, u32[]{:S(2)}) copy-start(bf16[1,2,16,512]{3,2,1,0:T(8,128)(2,1)} %param.13) | copy-start | bytes 98308
  28.6 4.0 %copy-start = (f32[1536,512]{1,0:T(8,128)S(1)}, f32[1536,512]{1,0:T(8,128)}, u32[]{:S(2)}) copy-start(f32[1536,512]{1,0:T(8,128)} %constant.13.clone) | copy-start | bytes 9437188
  34.5 14.8 %copy-start.3 = (f32[1,2,16,512]{3,2,1,0:T(8,128)S(1)}, f32[1,2,16,512]{3,2,1,0:T(8,128)}, u32[]{:S(2)}) copy-start(f32[1,2,16,512]{3,2,1,0:T(8,128)} %param.10) | copy-start | bytes 196612
  34.5 16.0 %copy-start.6 = (f32[1,2,16,512]{3,2,1,0:T(8,128)S(1)}, f32[1,2,16,512]{3,2,1,0:T(8,128)}, u32[]{:S(2)}) copy-start(f32[1,2,16,512]{3,2,1,0:T(8,128)} %param.9) | copy-start | bytes 196612
  35.0 3.7 %collective-permute-start.4 = (f32[1,1,2,16,1,8,8]{3,6,5,4,2,1,0:T(8,128)S(1)}, f32[1,1,2,16,1,8,8]{3,6,5,4,2,1,0:T(8,128)S(1)}, u32[]{:S(2)}, u32[]{:S(2)}) collective-permute-start(f32[1,1,2,16,1,8,8]{3,6,5,4,2,1,0:T(8,128)S(1)} %copy.48), channel_id=1, source_target_pairs={{0,8},{8,16},{16,24},{24,0},{1,9},{9,17},{17,25},{25,1},{2,10},{10... | collective-permute-start | bytes 24584 | tf_op jit(solution)/shard_map/ppermute | solution.py:29
  38.8 2.0 %collective-permute-start.5 = (f32[1,1,2,16,1,8,8]{3,6,5,4,2,1,0:T(8,128)S(1)}, f32[1,1,2,16,1,8,8]{3,6,5,4,2,1,0:T(8,128)S(1)}, u32[]{:S(2)}, u32[]{:S(2)}) collective-permute-start(f32[1,1,2,16,1,8,8]{3,6,5,4,2,1,0:T(8,128)S(1)} %get-tuple-element.37), channel_id=1, source_target_pairs={{8,0},{16,8},{24,16},{0,24},{9,1},{17,9},{25,17},{1,25},{10,2},{18... | collective-permute-start | bytes 24584 | tf_op jit(solution)/shard_map/ppermute | solution.py:30
  40.8 11.5 %copy-start.7 = (f32[8,8,8]{2,1,0:T(8,128)S(1)}, f32[8,8,8]{2,1,0:T(8,128)}, u32[]{:S(2)}) copy-start(f32[8,8,8]{2,1,0:T(8,128)} %constant.21) | copy-start | bytes 6148
  40.8 6.7 %collective-permute-start.6 = (f32[1,1,1,16,8,1,8]{3,6,5,4,2,1,0:T(8,128)S(1)}, f32[1,1,1,16,8,1,8]{3,6,5,4,2,1,0:T(8,128)S(1)}, u32[]{:S(2)}, u32[]{:S(2)}) collective-permute-start(f32[1,1,1,16,8,1,8]{3,6,5,4,2,1,0:T(8,128)S(1)} %pad_maximum_fusion.10), channel_id=1, source_target_pairs={{0,1},{1,2},{2,3},{3,4},{4,5},{5,6},{6,7},{7,0},{8,9},{9,10},{10,1... | collective-permute-start | bytes 12296 | tf_op jit(solution)/shard_map/ppermute | solution.py:29
  47.4 4.0 %collective-permute-start.7 = (f32[1,1,1,16,8,1,8]{3,6,5,4,2,1,0:T(8,128)S(1)}, f32[1,1,1,16,8,1,8]{3,6,5,4,2,1,0:T(8,128)S(1)}, u32[]{:S(2)}, u32[]{:S(2)}) collective-permute-start(f32[1,1,1,16,8,1,8]{3,6,5,4,2,1,0:T(8,128)S(1)} %get-tuple-element.21), channel_id=1, source_target_pairs={{1,0},{2,1},{3,2},{4,3},{5,4},{6,5},{7,6},{0,7},{9,8},{10,9},{11,1... | collective-permute-start | bytes 12296 | tf_op jit(solution)/shard_map/ppermute | solution.py:30
  50.7 2.6 %copy-start.1 = (f32[1,2,16,512]{2,3,1,0:T(8,128)S(1)}, f32[1,2,16,512]{2,3,1,0:T(8,128)}, u32[]{:S(2)}) copy-start(f32[1,2,16,512]{2,3,1,0:T(8,128)} %copy.36) | copy-start | bytes 196612
  99.2 3.6 %copy-start.2 = (f32[1,1,2,16,8,8,8]{3,6,5,4,2,1,0:T(8,128)S(1)}, f32[1,1,2,16,8,8,8]{3,6,5,4,2,1,0:T(8,128)}, u32[]{:S(2)}) copy-start(f32[1,1,2,16,8,8,8]{3,6,5,4,2,1,0:T(8,128)} %get-tuple-element.25) | copy-start | bytes 196612
where the time goes:
time: 104 us
  blocking collectives  40.2 us (39%)
  waiting for transfers between devices  28.1 us (27%)
  matrix products  8.94 us (9%)
  local copies, waits for them, and re-layouts  8.3 us (8%)
  starting transfers between devices  6.99 us (7%)
  other arithmetic  6.13 us (6%)
  between operations  4.95 us (5%)
    psum x1, blocking collectives, on_device(): lax.psum((jnp.sum(weights * residual * scaled), jnp.sum(weights * smooth...  40.2 us
    ppermute x4, waiting for transfers between devices, extended(): before = lax.ppermute(last, axis, up)  20.1 us
    dot_general x3, matrix products, highest(): jnp.dot(left, right, precision=lax.Precision.HIGHEST, preferred_element_t...  8.94 us
    ppermute x4, waiting for transfers between devices, extended(): after = lax.ppermute(initial, axis, down)  7.93 us
    unnamed x27, local copies, waits for them, and re-layouts  4.13 us
    ppermute x4, starting transfers between devices, extended(): after = lax.ppermute(initial, axis, down)  3.98 us
    ppermute x4, starting transfers between devices, extended(): before = lax.ppermute(last, axis, up)  3.01 us
  transfers between devices with their start and end apart: 8, of which 8 were waited for; matrix products, arithmetic and copies ran while one was open for 1% of the time, Pallas kernels for 0%

commit v1 on v0

v1 whole, which is shorter than its diff:
```python
import functools

import jax
import jax.numpy as jnp
import numpy as np
from jax import lax
from jax.experimental import pallas as pl
from jax.experimental.pallas import tpu as pltpu
from jax.sharding import PartitionSpec as P

NP = 8
LANES = 128
MESH = pl.DeviceIdType.MESH

lobatto_nodes = [
    -1.0,
    -0.8717401485096066,
    -0.5917001814331423,
    -0.2092992179024789,
    0.2092992179024789,
    0.5917001814331423,
    0.8717401485096066,
    1.0,
]


def derivative_table():
    nodes = np.array(lobatto_nodes)
    identity = np.eye(NP)
    offset = nodes[:, None] - nodes[None, :] + identity
    barycentric = 1.0 / np.prod(offset, axis=1)
    derivative = barycentric[None, :] / barycentric[:, None] / offset * (1.0 - identity)
    return derivative - identity * np.sum(derivative, axis=1)[:, None]


def split_table(table):
    table = np.asarray(table, np.float32)
    high = table.astype(jnp.bfloat16)
    low = (table - high.astype(np.float32)).astype(jnp.bfloat16)
    return high, low


def tables():
    d = derivative_table().astype(np.float32)
    along_j = np.kron(np.kron(np.eye(2), d), np.eye(NP))
    along_k = np.kron(np.eye(16), d)
    high, low = split_table(np.concatenate([along_j.T, along_k.T], axis=1))
    forward = np.concatenate([np.concatenate([high, high], 0), np.concatenate([low, low], 0)], 1)
    high, low = split_table(np.concatenate([along_j, along_k], axis=0))
    backward = np.concatenate([high, low], axis=1)
    high, low = split_table(np.concatenate([along_j * along_j, along_k * along_k], axis=0))
    squares = np.concatenate([high, low], axis=1)
    return np.concatenate([forward, backward, squares], axis=1)


def roll(x, shift):
    shift %= LANES
    return x if shift == 0 else pltpu.roll(x, shift, 1)


def lane_of(shape):
    return lax.broadcasted_iota(jnp.int32, shape, 1)


def along_i(table, blocks):
    low = lane_of(blocks[0].shape) < 64
    swapped = [roll(x, 64) for x in blocks]
    outs = []
    for b in range(4):
        total = None
        for c in range(4):
            same = jnp.where(low, float(table[2 * b, 2 * c]), float(table[2 * b + 1, 2 * c + 1]))
            other = jnp.where(low, float(table[2 * b, 2 * c + 1]), float(table[2 * b + 1, 2 * c]))
            term = same * blocks[c] + other * swapped[c]
            total = term if total is None else total + term
        outs.append(total)
    return outs


def weights_of(rows):
    lane = lane_of((rows, LANES))
    k, j = lane & 7, (lane >> 3) & 7
    half = lambda cond: jnp.where(cond, 0.5, 1.0)
    base = half((k == 0) | (k == 7)) * half((j == 0) | (j == 7))
    return [base * half(lane < 64), base, base, base * half(lane >= 64)]


def pack_i_face(x, side):
    h = x.shape[0] // 2
    top, bottom = x[:h], x[h:]
    low = lane_of(top.shape) < 64
    if side == 0:
        return jnp.where(low, top, roll(bottom, 64))
    return jnp.where(low, roll(top, 64), bottom)


def unpack_i_face(m, side):
    other = roll(m, 64)
    return jnp.concatenate([m, other] if side == 0 else [other, m], axis=0)


def pack_j_faces(fields, ez, side):
    lane = lane_of((ez, LANES))
    slot = (lane & 63) >> 3
    out = jnp.zeros((ez, LANES), jnp.float32)
    for n, blocks in enumerate(fields):
        for b in range(4):
            rows = blocks[b][:ez] if side == 0 else blocks[b][-ez:]
            moved = roll(rows, 8 * b + 32 * n - (0 if side == 0 else 56))
            out = jnp.where(slot == b + 4 * n, moved, out)
    return out


def join_j_faces(mine, before, after):
    lane = lane_of(mine.shape)
    first = (lane < 64) & ((lane & 31) < 8)
    last = (lane >= 64) & ((lane & 31) >= 24)
    return mine + jnp.where(first, roll(before, 40), jnp.where(last, roll(after, 88), 0.0))


def finish_assembly(blocks, n, ez, i_prev, i_next, j_prev, j_next):
    rows = blocks[0].shape[0]
    lane = lane_of((rows, LANES))
    low = lane < 64
    j, k = (lane >> 3) & 7, lane & 7
    blocks = list(blocks)
    blocks[0] = blocks[0] + jnp.where(low, unpack_i_face(i_prev, 0), 0.0)
    blocks[3] = blocks[3] + jnp.where(low, 0.0, unpack_i_face(i_next, 1))
    outs = []
    for b, x in enumerate(blocks):
        shift = 8 * b + 32 * n
        after, before = roll(j_next, 56 - shift), roll(j_prev, -shift)
        if rows > ez:
            after = jnp.concatenate([roll(x[ez:], 56), after], axis=0)
            before = jnp.concatenate([before, roll(x[:-ez], -56)], axis=0)
        x = x + jnp.where(j == 7, after, jnp.where(j == 0, before, 0.0))
        up, down = roll(x, 7), roll(x, -7)
        after = [pltpu.roll(up[e : e + ez], ez - 1, 0) for e in range(0, rows, ez)]
        before = [pltpu.roll(down[e : e + ez], 1, 0) for e in range(0, rows, ez)]
        after, before = jnp.concatenate(after, 0), jnp.concatenate(before, 0)
        outs.append(x + jnp.where(k == 7, after, jnp.where(k == 0, before, 0.0)))
    return outs


def halves(x):
    high = x.astype(jnp.bfloat16)
    return high, (x - high.astype(jnp.float32)).astype(jnp.bfloat16)


def dot(left, right):
    return jnp.dot(left, right, preferred_element_type=jnp.float32)


def stack(blocks):
    return jnp.concatenate(blocks, axis=0)


def total_of(blocks):
    x = blocks[0] + blocks[1] + (blocks[2] + blocks[3])
    return jnp.sum(jnp.sum(x, axis=0, keepdims=True), axis=1, keepdims=True)


def kernel(
    ng, nd, ez,
    sol_h, res_h, dir_h, geo_h, mass_h, tab_h,
    sol_o, res_o, dir_o,
    sol_v, res_v, dir_v, geo_v, mass_v, tab_v,
    i_out1, i_in1, j_out1, j_in1, i_out2, i_in2, j_out2, j_in2, part, parts,
    load_sem, send_sem, recv_sem, part_send, part_recv,
):
    me_g, me_d = lax.axis_index("group"), lax.axis_index("dev")

    def at(a, b):
        return (lax.rem(me_g + (a + ng), ng), lax.rem(me_d + (b + nd), nd))

    others = [(a, b) for a in range(ng) for b in range(nd) if (a, b) != (0, 0)]
    barrier = pltpu.get_barrier_semaphore()
    for a, b in others:
        pl.semaphore_signal(barrier, inc=1, device_id=at(a, b), device_id_type=MESH)

    pairs = ((dir_h, dir_v), (geo_h, geo_v), (mass_h, mass_v), (tab_h, tab_v), (res_h, res_v), (sol_h, sol_v))
    loads = [pltpu.make_async_copy(h, v, load_sem.at[n]) for n, (h, v) in enumerate(pairs)]
    for load in loads:
        load.start()

    rows = dir_v.shape[0]
    weights = weights_of(rows)
    cut = [slice(LANES * b, LANES * b + LANES) for b in range(4)]

    def exchange(phase, fields, i_out, i_in, j_out, j_in):
        h = rows // 2
        for n, blocks in enumerate(fields):
            i_out[0, n * h : (n + 1) * h] = pack_i_face(blocks[0], 0)
            i_out[1, n * h : (n + 1) * h] = pack_i_face(blocks[3], 1)
        for side in range(2):
            j_out[side] = pack_j_faces(fields, ez, side)
        copies = []
        for side, step in ((0, -1), (1, 1)):
            for turn, a in ((0, -1), (1, 0), (2, 1)):
                copies.append((j_out.at[side], j_in.at[side, turn], at(a, step)))
            copies.append((i_out.at[side], i_in.at[side], at(step, 0)))
        made = []
        for n, (src, dst, target) in enumerate(copies):
            made.append(
                pltpu.make_async_remote_copy(
                    src_ref=src, dst_ref=dst,
                    send_sem=send_sem.at[phase, n], recv_sem=recv_sem.at[phase, n],
                    device_id=target, device_id_type=MESH,
                )
            )
        return made

    def assembled(fields, i_in, j_in):
        h = rows // 2
        j_prev = join_j_faces(j_in[1, 1], j_in[1, 2], j_in[1, 0])
        j_next = join_j_faces(j_in[0, 1], j_in[0, 2], j_in[0, 0])
        return [
            finish_assembly(
                blocks, n, ez,
                i_in[1, n * h : (n + 1) * h], i_in[0, n * h : (n + 1) * h], j_prev, j_next,
            )
            for n, blocks in enumerate(fields)
        ]

    d = derivative_table().astype(np.float32)
    loads[0].wait()
    weighted = [weights[b] * dir_v[:, cut[b]] for b in range(4)]
    for load in loads[1:4]:
        load.wait()
    geo_rows = stack([jnp.concatenate([geo_v[1, :, c], geo_v[2, :, c]], axis=1) for c in cut])
    squared = dot(geo_rows, tab_v[:, 768:1024])
    squared = squared[:, :LANES] + squared[:, LANES:]
    geo = [[geo_v[c, :, cut[b]].astype(jnp.float32) for b in range(4)] for c in range(3)]
    mass = [mass_v[:, c].astype(jnp.float32) for c in cut]
    diag = along_i((d * d).T, geo[0])
    diag = [diag[b] + squared[rows * b : rows * b + rows] + mass[b] for b in range(4)]
    first = exchange(0, (weighted, diag), i_out1, i_in1, j_out1, j_in1)
    pl.semaphore_wait(barrier, len(others))
    for copy in first:
        copy.start()
    loads[4].wait()
    loads[5].wait()
    for copy in first:
        copy.wait_recv()
    smooth, diagonal = assembled((weighted, diag), i_in1, j_in1)

    high, low = halves(stack(smooth))
    grads = dot(jnp.concatenate([high, low], axis=1), tab_v[:, :512])
    grads = grads[:, :256] + grads[:, 256:]
    grad_i = along_i(d, smooth)
    flux_i = [geo[0][b] * grad_i[b] for b in range(4)]
    flux = jnp.concatenate(
        [stack(geo[1]) * grads[:, :LANES], stack(geo[2]) * grads[:, LANES:]], axis=1
    )
    high, low = halves(flux)
    back = dot(jnp.concatenate([high, low], axis=0), tab_v[:, 512:768])
    back = back[: 4 * rows] + back[4 * rows :]
    back = back[:, :LANES] + back[:, LANES:]
    local = along_i(d.T, flux_i)
    local = [local[b] + back[rows * b : rows * b + rows] + mass[b] * smooth[b] for b in range(4)]

    second = exchange(1, (local,), i_out2, i_in2, j_out2, j_in2)
    for copy in second:
        copy.start()
    inverse = [1.0 / x for x in diagonal]
    residual = [res_v[:, c] for c in cut]
    scaled = [residual[b] * inverse[b] for b in range(4)]
    norm_now = total_of([weights[b] * residual[b] * scaled[b] for b in range(4)])
    curvature = total_of([smooth[b] * local[b] for b in range(4)])
    for copy in second:
        copy.wait_recv()
    (applied,) = assembled((local,), i_in2, j_in2)
    shared = [weights[b] * applied[b] for b in range(4)]
    cross = total_of([shared[b] * scaled[b] for b in range(4)])
    quad = total_of([shared[b] * applied[b] * inverse[b] for b in range(4)])

    lane = lane_of((1, LANES))
    mine = jnp.where(
        lane < 32, norm_now, jnp.where(lane < 64, curvature, jnp.where(lane < 96, cross, quad))
    )
    part[0] = mine
    for n, (a, b) in enumerate(others):
        pltpu.make_async_remote_copy(
            src_ref=part.at[0], dst_ref=parts.at[n],
            send_sem=part_send, recv_sem=part_recv,
            device_id=at(a, b), device_id_type=MESH,
        ).start()
    pltpu.make_async_copy(parts, parts, part_recv).wait()
    everyone = mine + jnp.sum(parts[...], axis=0)
    norm_now, curvature, cross, quad = (everyone[:, 32 * n : 32 * n + 1] for n in range(4))
    step = norm_now / curvature
    norm_next = norm_now - 2.0 * step * cross + step * step * quad
    ratio = norm_next / norm_now
    for b, c in enumerate(cut):
        sol_o[:, c] = sol_v[:, c] + step * smooth[b]
        out = residual[b] - step * applied[b]
        res_o[:, c] = out
        dir_o[:, c] = out * inverse[b] + ratio * smooth[b]
    for copy in first + second:
        copy.wait_send()
    pltpu.make_async_copy(parts, parts, part_send).wait()


def on_device(solution, residual, direction, geometry, mass):
    dims = solution.shape
    ng, nd = lax.axis_size("group"), lax.axis_size("dev")
    ez, points = dims[2], dims[3]
    rows = dims[0] * dims[1] * ez
    flat = (rows, points)
    f32, bf16 = jnp.float32, jnp.bfloat16
    table = jnp.asarray(tables())
    h = rows // 2
    outs = pl.pallas_call(
        functools.partial(kernel, ng, nd, ez),
        out_shape=[jax.ShapeDtypeStruct(flat, f32)] * 3,
        in_specs=[pl.BlockSpec(memory_space=pl.ANY)] * 6,
        out_specs=[pl.BlockSpec(memory_space=pltpu.VMEM)] * 3,
        scratch_shapes=[
            pltpu.VMEM(flat, f32),
            pltpu.VMEM(flat, f32),
            pltpu.VMEM(flat, f32),
            pltpu.VMEM((3,) + flat, bf16),
            pltpu.VMEM(flat, bf16),
            pltpu.VMEM(table.shape, bf16),
            pltpu.VMEM((2, 2 * h, LANES), f32),
            pltpu.VMEM((2, 2 * h, LANES), f32),
            pltpu.VMEM((2, ez, LANES), f32),
            pltpu.VMEM((2, 3, ez, LANES), f32),
            pltpu.VMEM((2, h, LANES), f32),
            pltpu.VMEM((2, h, LANES), f32),
            pltpu.VMEM((2, ez, LANES), f32),
            pltpu.VMEM((2, 3, ez, LANES), f32),
            pltpu.VMEM((1, 1, LANES), f32),
            pltpu.VMEM((ng * nd - 1, 1, LANES), f32),
            pltpu.SemaphoreType.DMA((6,)),
            pltpu.SemaphoreType.DMA((2, 8)),
            pltpu.SemaphoreType.DMA((2, 8)),
            pltpu.SemaphoreType.DMA,
            pltpu.SemaphoreType.DMA,
        ],
        compiler_params=pltpu.CompilerParams(collective_id=0, has_side_effects=True),
    )(
        solution.reshape(flat),
        residual.reshape(flat),
        direction.reshape(flat),
        geometry.reshape((3,) + flat),
        mass.reshape(flat),
        table,
    )
    return tuple(x.reshape(dims) for x in outs)


def solution(mesh):
    spec = P("group", "dev", None, None)
    return jax.shard_map(
        on_device,
        mesh=mesh,
        in_specs=(spec, spec, spec, P(None, "group", "dev", None, None), spec),
        out_specs=(spec, spec, spec),
        check_vma=False,
    )
```

time: 104 us -> 24.5 us (0.24)
  blocking collectives: 40.2 us -> 0 us
  waiting for transfers between devices: 28.1 us -> 0 us
  Pallas kernels: 0 us -> 20.6 us
  matrix products: 8.94 us -> 0 us
  starting transfers between devices: 6.99 us -> 0 us
  other arithmetic: 6.13 us -> 0 us
  local copies, waits for them, and re-layouts: 8.3 us -> 3 us
  between operations: 4.95 us -> 0.65 us
    psum x1 -> x0, blocking collectives: 40.2 us -> none  [on_device(): lax.psum((jnp.sum(weights * residual * scaled), jnp.sum(weights * smooth...]
    ppermute x8 -> x0, waiting for transfers between devices: 28.1 us -> none  [the longest x4 20.1 us: extended(): before = lax.ppermute(last, axis, up)]
    pallas_call x0 -> x1, Pallas kernels: none -> 20.6 us  [on_device(): pl.pallas_call(functools.partial(kernel, ng, nd, ez), out_shape=[jax.Shap...]
    dot_general x3 -> x0, matrix products: 8.94 us -> none  [highest(): jnp.dot(left, right, precision=lax.Precision.HIGHEST, preferred_element_t...]
    ppermute x8 -> x0, starting transfers between devices: 6.99 us -> none  [the longest x4 3.98 us: extended(): after = lax.ppermute(initial, axis, down)]
    add x14 -> x0, other arithmetic: 2.46 us -> none  [the longest x1 0.91 us: on_device(): direction_out = residual_out / diagonal + norm_next / norm_now * smooth]
    reduce_sum x2 -> x0, other arithmetic: 1.91 us -> none  [the longest x1 1.07 us: on_device(): jnp.sum(weights * applied * applied / diagonal)]
    unnamed x27 -> x7, local copies, waits for them, and re-layouts: 4.13 us -> 3 us
  transfers between devices with their start and end apart: 8 -> 0, of which waited for: 8 -> 0; matrix products, arithmetic and copies ran while one was open for 1% -> 0% of each run, Pallas kernels for 0% -> 0%
where the time goes in v1:
time: 24.5 us; the launch traced here: 24.3 us
  Pallas kernels  20.6 us (84%)
  local copies, waits for them, and re-layouts  3 us (12%)
  between operations  0.65 us (3%)
    pallas_call x1, Pallas kernels, on_device(): pl.pallas_call(functools.partial(kernel, ng, nd, ez), out_shape=[jax.Shap...  20.6 us
    unnamed x7, local copies, waits for them, and re-layouts  3 us

profile of v1, /device:TPU:0, one launch (start us, length us, event | category | flops | bytes accessed | tf_op | source)
XLA Modules:
  0.0 24.3 jit_solution(1856839186456824982)
XLA Ops:
  0.6 20.6 %shard_map.85 = (f32[32,512]{1,0:T(8,128)}, f32[32,512]{1,0:T(8,128)}, f32[32,512]{1,0:T(8,128)}) custom-call(f32[32,512]{1,0:T(8,128)} %bitcast.12, f32[32,512]{1,0:T(8,128)} %bitcast.13, f32[32,512]{1,0:T(8,128)} %bitcast.14, bf16[3,32,512]{2,1,0:T(8,128)(2,1)} %bitcast.8, bf16[32,512]{1,0:T(8,128)(2,1)} %bitcast.15, bf16[256,1024]{1,0:T(8,128)(2,1)} %constant.2.clone.tab_h), custom_call_target="tpu_custom_call" | custom-call | tf_op jit(solution)/shard_map/pallas_call | solution.py:313
  21.3 0.0 copy-start.1
  21.3 1.5 %copy.12 = f32[1,2,16,512]{3,2,1,0:T(8,128)} copy(f32[1,2,16,512]{3,2,1,0:T(8,128)} %bitcast.11) | data formatting | bytes 131072
  22.8 0.0 copy-done.1
  22.8 0.0 copy-start
  22.8 0.6 %copy.13 = f32[1,2,16,512]{3,2,1,0:T(8,128)} copy(f32[1,2,16,512]{3,2,1,0:T(8,128)S(1)} %bitcast.10) | data formatting | bytes 131072
  23.4 0.2 copy-done
  23.7 0.6 %copy.14 = f32[1,2,16,512]{3,2,1,0:T(8,128)} copy(f32[1,2,16,512]{3,2,1,0:T(8,128)S(1)} %bitcast.9) | data formatting | bytes 131072
Async XLA Ops:
  21.3 1.5 %copy-start.1 = (f32[32,512]{1,0:T(8,128)S(1)}, f32[32,512]{1,0:T(8,128)}, u32[]{:S(2)}) copy-start(f32[32,512]{1,0:T(8,128)} %get-tuple-element.7) | copy-start | bytes 196612
  22.8 0.9 %copy-start = (f32[32,512]{1,0:T(8,128)S(1)}, f32[32,512]{1,0:T(8,128)}, u32[]{:S(2)}) copy-start(f32[32,512]{1,0:T(8,128)} %get-tuple-element.8) | copy-start | bytes 196612

commit v2 on v1

--- a/solution.py
+++ b/solution.py
@@ -99,16 +99,21 @@
     return jnp.concatenate([m, other] if side == 0 else [other, m], axis=0)
 
 
-def pack_j_faces(fields, ez, side):
-    lane = lane_of((ez, LANES))
+def pack_j_face(blocks, ez, side):
+    half = ez // 2
+    lane = lane_of((half, LANES))
     slot = (lane & 63) >> 3
-    out = jnp.zeros((ez, LANES), jnp.float32)
-    for n, blocks in enumerate(fields):
-        for b in range(4):
-            rows = blocks[b][:ez] if side == 0 else blocks[b][-ez:]
-            moved = roll(rows, 8 * b + 32 * n - (0 if side == 0 else 56))
+    out = jnp.zeros((half, LANES), jnp.float32)
+    for b in range(4):
+        rows = blocks[b][:ez] if side == 0 else blocks[b][-ez:]
+        for n in range(2):
+            moved = roll(rows[n * half : (n + 1) * half], 8 * b + 32 * n - (0 if side == 0 else 56))
             out = jnp.where(slot == b + 4 * n, moved, out)
     return out
+
+
+def unpack_j_face(m, b, shift):
+    return jnp.concatenate([roll(m, shift - 8 * b), roll(m, shift - 8 * b - 32)], axis=0)
 
 
 def join_j_faces(mine, before, after):
@@ -118,7 +123,7 @@
     return mine + jnp.where(first, roll(before, 40), jnp.where(last, roll(after, 88), 0.0))
 
 
-def finish_assembly(blocks, n, ez, i_prev, i_next, j_prev, j_next):
+def finish_assembly(blocks, ez, i_prev, i_next, j_prev, j_next):
     rows = blocks[0].shape[0]
     lane = lane_of((rows, LANES))
     low = lane < 64
@@ -128,8 +133,7 @@
     blocks[3] = blocks[3] + jnp.where(low, 0.0, unpack_i_face(i_next, 1))
     outs = []
     for b, x in enumerate(blocks):
-        shift = 8 * b + 32 * n
-        after, before = roll(j_next, 56 - shift), roll(j_prev, -shift)
+        after, before = unpack_j_face(j_next, b, 56), unpack_j_face(j_prev, b, 0)
         if rows > ez:
             after = jnp.concatenate([roll(x[ez:], 56), after], axis=0)
             before = jnp.concatenate([before, roll(x[:-ez], -56)], axis=0)
@@ -165,7 +169,7 @@
     sol_h, res_h, dir_h, geo_h, mass_h, tab_h,
     sol_o, res_o, dir_o,
     sol_v, res_v, dir_v, geo_v, mass_v, tab_v,
-    i_out1, i_in1, j_out1, j_in1, i_out2, i_in2, j_out2, j_in2, part, parts,
+    i_out, i_in, j_out, j_in, part, parts,
     load_sem, send_sem, recv_sem, part_send, part_recv,
 ):
     me_g, me_d = lax.axis_index("group"), lax.axis_index("dev")
@@ -187,44 +191,36 @@
     weights = weights_of(rows)
     cut = [slice(LANES * b, LANES * b + LANES) for b in range(4)]
 
-    def exchange(phase, fields, i_out, i_in, j_out, j_in):
-        h = rows // 2
-        for n, blocks in enumerate(fields):
-            i_out[0, n * h : (n + 1) * h] = pack_i_face(blocks[0], 0)
-            i_out[1, n * h : (n + 1) * h] = pack_i_face(blocks[3], 1)
-        for side in range(2):
-            j_out[side] = pack_j_faces(fields, ez, side)
+    def exchange(phase, blocks):
         copies = []
         for side, step in ((0, -1), (1, 1)):
-            for turn, a in ((0, -1), (1, 0), (2, 1)):
-                copies.append((j_out.at[side], j_in.at[side, turn], at(a, step)))
-            copies.append((i_out.at[side], i_in.at[side], at(step, 0)))
-        made = []
-        for n, (src, dst, target) in enumerate(copies):
-            made.append(
-                pltpu.make_async_remote_copy(
-                    src_ref=src, dst_ref=dst,
-                    send_sem=send_sem.at[phase, n], recv_sem=recv_sem.at[phase, n],
-                    device_id=target, device_id_type=MESH,
-                )
+            j_out[phase, side] = pack_j_face(blocks, ez, side)
+            for turn, a in ((1, 0), (0, -1), (2, 1)):
+                copies.append((j_out.at[phase, side], j_in.at[phase, side, turn], at(a, step)))
+        for side, step in ((0, -1), (1, 1)):
+            i_out[phase, side] = pack_i_face(blocks[3 * side], side)
+            copies.append((i_out.at[phase, side], i_in.at[phase, side], at(step, 0)))
+        return [
+            pltpu.make_async_remote_copy(
+                src_ref=src, dst_ref=dst,
+                send_sem=send_sem.at[phase, n], recv_sem=recv_sem.at[phase, n],
+                device_id=target, device_id_type=MESH,
             )
-        return made
-
-    def assembled(fields, i_in, j_in):
-        h = rows // 2
-        j_prev = join_j_faces(j_in[1, 1], j_in[1, 2], j_in[1, 0])
-        j_next = join_j_faces(j_in[0, 1], j_in[0, 2], j_in[0, 0])
-        return [
-            finish_assembly(
-                blocks, n, ez,
-                i_in[1, n * h : (n + 1) * h], i_in[0, n * h : (n + 1) * h], j_prev, j_next,
-            )
-            for n, blocks in enumerate(fields)
+            for n, (src, dst, target) in enumerate(copies)
         ]
+
+    def assembled(phase, blocks):
+        j_prev = join_j_faces(j_in[phase, 1, 1], j_in[phase, 1, 2], j_in[phase, 1, 0])
+        j_next = join_j_faces(j_in[phase, 0, 1], j_in[phase, 0, 2], j_in[phase, 0, 0])
+        return finish_assembly(blocks, ez, i_in[phase, 1], i_in[phase, 0], j_prev, j_next)
 
     d = derivative_table().astype(np.float32)
     loads[0].wait()
     weighted = [weights[b] * dir_v[:, cut[b]] for b in range(4)]
+    first = exchange(0, weighted)
+    pl.semaphore_wait(barrier, len(others))
+    for copy in first:
+        copy.start()
     for load in loads[1:4]:
         load.wait()
     geo_rows = stack([jnp.concatenate([geo_v[1, :, c], geo_v[2, :, c]], axis=1) for c in cut])
@@ -234,15 +230,14 @@
     mass = [mass_v[:, c].astype(jnp.float32) for c in cut]
     diag = along_i((d * d).T, geo[0])
     diag = [diag[b] + squared[rows * b : rows * b + rows] + mass[b] for b in range(4)]
-    first = exchange(0, (weighted, diag), i_out1, i_in1, j_out1, j_in1)
-    pl.semaphore_wait(barrier, len(others))
-    for copy in first:
+    side_copies = exchange(1, diag)
+    for copy in side_copies:
         copy.start()
     loads[4].wait()
     loads[5].wait()
     for copy in first:
         copy.wait_recv()
-    smooth, diagonal = assembled((weighted, diag), i_in1, j_in1)
+    smooth = assembled(0, weighted)
 
     high, low = halves(stack(smooth))
     grads = dot(jnp.concatenate([high, low], axis=1), tab_v[:, :512])
@@ -259,17 +254,19 @@
     local = along_i(d.T, flux_i)
     local = [local[b] + back[rows * b : rows * b + rows] + mass[b] * smooth[b] for b in range(4)]
 
-    second = exchange(1, (local,), i_out2, i_in2, j_out2, j_in2)
+    second = exchange(2, local)
     for copy in second:
         copy.start()
-    inverse = [1.0 / x for x in diagonal]
+    for copy in side_copies:
+        copy.wait_recv()
+    inverse = [1.0 / x for x in assembled(1, diag)]
     residual = [res_v[:, c] for c in cut]
     scaled = [residual[b] * inverse[b] for b in range(4)]
     norm_now = total_of([weights[b] * residual[b] * scaled[b] for b in range(4)])
     curvature = total_of([smooth[b] * local[b] for b in range(4)])
     for copy in second:
         copy.wait_recv()
-    (applied,) = assembled((local,), i_in2, j_in2)
+    applied = assembled(2, local)
     shared = [weights[b] * applied[b] for b in range(4)]
     cross = total_of([shared[b] * scaled[b] for b in range(4)])
     quad = total_of([shared[b] * applied[b] * inverse[b] for b in range(4)])
@@ -296,9 +293,17 @@
         out = residual[b] - step * applied[b]
         res_o[:, c] = out
         dir_o[:, c] = out * inverse[b] + ratio * smooth[b]
-    for copy in first + second:
+    for copy in first + side_copies + second:
         copy.wait_send()
     pltpu.make_async_copy(parts, parts, part_send).wait()
+
+
+def deliver(*refs):
+    copies = [pltpu.make_async_copy(refs[n], refs[3 + n], refs[6].at[n]) for n in range(3)]
+    for copy in copies:
+        copy.start()
+    for copy in copies:
+        copy.wait()
 
 
 def on_device(solution, residual, direction, geometry, mass):
@@ -312,8 +317,8 @@
     h = rows // 2
     outs = pl.pallas_call(
         functools.partial(kernel, ng, nd, ez),
-        out_shape=[jax.ShapeDtypeStruct(flat, f32)] * 3,
-        in_specs=[pl.BlockSpec(memory_space=pl.ANY)] * 6,
+        out_shape=[pltpu.VMEM(flat, f32)] * 3,
+        in_specs=[pl.BlockSpec(memory_space=pltpu.HBM)] * 6,
         out_specs=[pl.BlockSpec(memory_space=pltpu.VMEM)] * 3,
         scratch_shapes=[
             pltpu.VMEM(flat, f32),
@@ -322,31 +327,35 @@
             pltpu.VMEM((3,) + flat, bf16),
             pltpu.VMEM(flat, bf16),
             pltpu.VMEM(table.shape, bf16),
-            pltpu.VMEM((2, 2 * h, LANES), f32),
-            pltpu.VMEM((2, 2 * h, LANES), f32),
-            pltpu.VMEM((2, ez, LANES), f32),
-            pltpu.VMEM((2, 3, ez, LANES), f32),
-            pltpu.VMEM((2, h, LANES), f32),
-            pltpu.VMEM((2, h, LANES), f32),
-            pltpu.VMEM((2, ez, LANES), f32),
-            pltpu.VMEM((2, 3, ez, LANES), f32),
+            pltpu.VMEM((3, 2, h, LANES), f32),
+            pltpu.VMEM((3, 2, h, LANES), f32),
+            pltpu.VMEM((3, 2, ez // 2, LANES), f32),
+            pltpu.VMEM((3, 2, 3, ez // 2, LANES), f32),
             pltpu.VMEM((1, 1, LANES), f32),
             pltpu.VMEM((ng * nd - 1, 1, LANES), f32),
             pltpu.SemaphoreType.DMA((6,)),
-            pltpu.SemaphoreType.DMA((2, 8)),
-            pltpu.SemaphoreType.DMA((2, 8)),
+            pltpu.SemaphoreType.DMA((3, 8)),
+            pltpu.SemaphoreType.DMA((3, 8)),
             pltpu.SemaphoreType.DMA,
             pltpu.SemaphoreType.DMA,
         ],
-        compiler_params=pltpu.CompilerParams(collective_id=0, has_side_effects=True),
+        compiler_params=pltpu.CompilerParams(collective_id=0, has_side_effects=True, vmem_limit_bytes=8 << 20),
     )(
-        solution.reshape(flat),
-        residual.reshape(flat),
-        direction.reshape(flat),
-        geometry.reshape((3,) + flat),
-        mass.reshape(flat),
-        table,
+        pltpu.with_memory_space_constraint(solution.reshape(flat), pltpu.HBM),
+        pltpu.with_memory_space_constraint(residual.reshape(flat), pltpu.HBM),
+        pltpu.with_memory_space_constraint(direction.reshape(flat), pltpu.HBM),
+        pltpu.with_memory_space_constraint(geometry.reshape((3,) + flat), pltpu.HBM),
+        pltpu.with_memory_space_constraint(mass.reshape(flat), pltpu.HBM),
+        pltpu.with_memory_space_constraint(table, pltpu.HBM),
     )
+    outs = pl.pallas_call(
+        deliver,
+        out_shape=[jax.ShapeDtypeStruct(flat, f32)] * 3,
+        in_specs=[pl.BlockSpec(memory_space=pl.ANY)] * 3,
+        out_specs=[pl.BlockSpec(memory_space=pltpu.HBM)] * 3,
+        scratch_shapes=[pltpu.SemaphoreType.DMA((3,))],
+        compiler_params=pltpu.CompilerParams(vmem_limit_bytes=8 << 20),
+    )(*outs)
     return tuple(x.reshape(dims) for x in outs)
 
 

time: 24.5 us -> 21 us (0.86)
  local copies, waits for them, and re-layouts: 3 us -> 0 us
  Pallas kernels: 20.6 us -> 20.3 us
    unnamed x7 -> x0, local copies, waits for them, and re-layouts: 3 us -> none
    pallas_call x1 -> x2, Pallas kernels: 20.6 us -> 20.3 us  [the longest x1 19.6 us: on_device(): pl.pallas_call(functools.partial(kernel, ng, nd, ez), out_shape=[pltpu.VM...]
where the time goes in v2:
time: 21 us; the launch traced here: 20.9 us
  Pallas kernels  20.3 us (97%)
  between operations  0.64 us (3%)
    pallas_call x1, Pallas kernels, on_device(): pl.pallas_call(functools.partial(kernel, ng, nd, ez), out_shape=[pltpu.VM...  19.6 us
    pallas_call x1, Pallas kernels, on_device(): pl.pallas_call(deliver, out_shape=[jax.ShapeDtypeStruct(flat, f32)] * 3,...  0.7 us

profile of v2, /device:TPU:0, one launch (start us, length us, event | category | flops | bytes accessed | tf_op | source)
XLA Modules:
  0.0 20.9 jit_solution(17409885799347731588)
XLA Ops:
  0.6 19.6 %shard_map.85 = (f32[32,512]{1,0:T(8,128)S(1)}, f32[32,512]{1,0:T(8,128)S(1)}, f32[32,512]{1,0:T(8,128)S(1)}) custom-call(f32[32,512]{1,0:T(8,128)} %bitcast.9, f32[32,512]{1,0:T(8,128)} %bitcast.10, f32[32,512]{1,0:T(8,128)} %bitcast.11, bf16[3,32,512]{2,1,0:T(8,128)(2,1)} %bitcast.8, bf16[32,512]{1,0:T(8,128)(2,1)} %bitcast.12, ...), custom_call_target="tpu_custom_call" | custom-call | tf_op jit(solution)/shard_map/pallas_call | solution.py:318
  20.2 0.7 %shard_map.86 = (f32[32,512]{1,0:T(8,128)}, f32[32,512]{1,0:T(8,128)}, f32[32,512]{1,0:T(8,128)}) custom-call(f32[32,512]{1,0:T(8,128)S(1)} %get-tuple-element.9.refs_0_, f32[32,512]{1,0:T(8,128)S(1)} %get-tuple-element.10.refs_1_, f32[32,512]{1,0:T(8,128)S(1)} %get-tuple-element.11.refs_2_), custom_call_target="tpu_custom_call" | custom-call | tf_op jit(solution)/shard_map/pallas_call | solution.py:351

commit v3 on v2

--- a/solution.py
+++ b/solution.py
@@ -178,6 +178,7 @@
         return (lax.rem(me_g + (a + ng), ng), lax.rem(me_d + (b + nd), nd))
 
     others = [(a, b) for a in range(ng) for b in range(nd) if (a, b) != (0, 0)]
+    others.sort(key=lambda t: (min(t[1], nd - t[1]) != 1, min(t[0], ng - t[0]) > 1))
     barrier = pltpu.get_barrier_semaphore()
     for a, b in others:
         pl.semaphore_signal(barrier, inc=1, device_id=at(a, b), device_id_type=MESH)
@@ -191,23 +192,29 @@
     weights = weights_of(rows)
     cut = [slice(LANES * b, LANES * b + LANES) for b in range(4)]
 
-    def exchange(phase, blocks):
-        copies = []
-        for side, step in ((0, -1), (1, 1)):
-            j_out[phase, side] = pack_j_face(blocks, ez, side)
-            for turn, a in ((1, 0), (0, -1), (2, 1)):
-                copies.append((j_out.at[phase, side], j_in.at[phase, side, turn], at(a, step)))
+    def exchange(phase, blocks, started=True):
+        made = []
+
+        def give(src, dst, target):
+            n = len(made)
+            made.append(
+                pltpu.make_async_remote_copy(
+                    src_ref=src, dst_ref=dst,
+                    send_sem=send_sem.at[phase, n], recv_sem=recv_sem.at[phase, n],
+                    device_id=target, device_id_type=MESH,
+                )
+            )
+            if started:
+                made[-1].start()
+
         for side, step in ((0, -1), (1, 1)):
             i_out[phase, side] = pack_i_face(blocks[3 * side], side)
-            copies.append((i_out.at[phase, side], i_in.at[phase, side], at(step, 0)))
-        return [
-            pltpu.make_async_remote_copy(
-                src_ref=src, dst_ref=dst,
-                send_sem=send_sem.at[phase, n], recv_sem=recv_sem.at[phase, n],
-                device_id=target, device_id_type=MESH,
-            )
-            for n, (src, dst, target) in enumerate(copies)
-        ]
+            give(i_out.at[phase, side], i_in.at[phase, side], at(step, 0))
+        for side, step in ((1, 1), (0, -1)):
+            j_out[phase, side] = pack_j_face(blocks, ez, side)
+            for turn, a in ((0, -1), (2, 1), (1, 0)):
+                give(j_out.at[phase, side], j_in.at[phase, side, turn], at(a, step))
+        return made
 
     def assembled(phase, blocks):
         j_prev = join_j_faces(j_in[phase, 1, 1], j_in[phase, 1, 2], j_in[phase, 1, 0])
@@ -217,7 +224,7 @@
     d = derivative_table().astype(np.float32)
     loads[0].wait()
     weighted = [weights[b] * dir_v[:, cut[b]] for b in range(4)]
-    first = exchange(0, weighted)
+    first = exchange(0, weighted, started=False)
     pl.semaphore_wait(barrier, len(others))
     for copy in first:
         copy.start()
@@ -231,8 +238,6 @@
     diag = along_i((d * d).T, geo[0])
     diag = [diag[b] + squared[rows * b : rows * b + rows] + mass[b] for b in range(4)]
     side_copies = exchange(1, diag)
-    for copy in side_copies:
-        copy.start()
     loads[4].wait()
     loads[5].wait()
     for copy in first:
@@ -255,8 +260,6 @@
     local = [local[b] + back[rows * b : rows * b + rows] + mass[b] * smooth[b] for b in range(4)]
 
     second = exchange(2, local)
-    for copy in second:
-        copy.start()
     for copy in side_copies:
         copy.wait_recv()
     inverse = [1.0 / x for x in assembled(1, diag)]

time: 21 us -> 21 us (level)
  no operation moved by 1% of the time
where the time goes in v3:
time: 21 us; the launch traced here: 20.9 us
  Pallas kernels  20.2 us (96%)
  between operations  0.64 us (3%)
    pallas_call x1, Pallas kernels, on_device(): pl.pallas_call(functools.partial(kernel, ng, nd, ez), out_shape=[pltpu.VM...  19.5 us
    pallas_call x1, Pallas kernels, on_device(): pl.pallas_call(deliver, out_shape=[jax.ShapeDtypeStruct(flat, f32)] * 3,...  0.7 us

profile of v3, /device:TPU:0, one launch (start us, length us, event | category | flops | bytes accessed | tf_op | source)
XLA Modules:
  0.0 20.9 jit_solution(12734376420679152910)
XLA Ops:
  0.6 19.5 %shard_map.85 = (f32[32,512]{1,0:T(8,128)S(1)}, f32[32,512]{1,0:T(8,128)S(1)}, f32[32,512]{1,0:T(8,128)S(1)}) custom-call(f32[32,512]{1,0:T(8,128)} %bitcast.9, f32[32,512]{1,0:T(8,128)} %bitcast.10, f32[32,512]{1,0:T(8,128)} %bitcast.11, bf16[3,32,512]{2,1,0:T(8,128)(2,1)} %bitcast.8, bf16[32,512]{1,0:T(8,128)(2,1)} %bitcast.12, ...), custom_call_target="tpu_custom_call" | custom-call | tf_op jit(solution)/shard_map/pallas_call | solution.py:321
  20.2 0.7 %shard_map.86 = (f32[32,512]{1,0:T(8,128)}, f32[32,512]{1,0:T(8,128)}, f32[32,512]{1,0:T(8,128)}) custom-call(f32[32,512]{1,0:T(8,128)S(1)} %get-tuple-element.9.refs_0_, f32[32,512]{1,0:T(8,128)S(1)} %get-tuple-element.10.refs_1_, f32[32,512]{1,0:T(8,128)S(1)} %get-tuple-element.11.refs_2_), custom_call_target="tpu_custom_call" | custom-call | tf_op jit(solution)/shard_map/pallas_call | solution.py:354
